TPU v7x, 32 devices: a whole 2x2x4 slice. The times are simulated.
32 devices in a mesh: grp: 4 (over z), dp: 2 (over x), tp: 4 (over y, core).
Axes of the slice: x: 2, y: 2, z: 4, core: 2. Of those that a mesh axis runs over, the one named last changes fastest.
Arguments:
- hidden_last: bfloat16 [128, 5120], P(('grp', 'dp')), may hold values from -6 to 6
- gain: float32 [5120], replicated, may hold values from 0.25 to 1.75
- w_query: bfloat16 [5120, 2560], P('dp', 'tp'), may hold values from -0.078125 to 0.078125
- w_key: bfloat16 [5120, 512], P('dp', 'tp'), may hold values from -0.078125 to 0.078125
- w_value: bfloat16 [5120, 512], P('dp', 'tp'), may hold values from -0.078125 to 0.078125
- w_out: bfloat16 [2560, 5120], P('tp'), may hold values from -0.125 to 0.125
- cache_keys: bfloat16 [128, 128, 512], P(('grp', 'dp'), None, 'tp'), may hold values from -6 to 6
- cache_values: bfloat16 [128, 128, 512], P(('grp', 'dp'), None, 'tp'), may hold values from -6 to 6
- cache_lengths: int32 [128], P(('grp', 'dp')), may hold values from 1 to 128
- reward_vec: float32 [5120], replicated, may hold values from -0.078125 to 0.078125
- response_counts: int32 [128], P('grp'), may hold values from 4 to 16
- assignment: int32 [128], P('grp'), may hold values from 0 to 1, as said below
- responses: bfloat16 [128, 16, 5120], P(('grp', 'dp'), None, 'tp'), may hold values from -6 to 6
- cotangent: bfloat16 [128, 16, 5120], P(('grp', 'dp'), None, 'tp'), may hold values from -6 to 6
Outputs:
- decoded: bfloat16 [128, 5120], P(('grp', 'dp'))
- advantage: float32 [128], P(('grp', 'dp'))
- layer_out: bfloat16 [128, 16, 5120], P(('grp', 'dp'), None, 'tp')
- grad_query: float32 [5120, 2560], P('dp', 'tp')
- grad_key: float32 [5120, 512], P('dp', 'tp')
- grad_value: float32 [5120, 512], P('dp', 'tp')
Inputs may be any that keep to these rules, and one draw needn't show every extreme that they name: `assignment`: within each group, every training shard receives exactly 16 rows, and from the 16 rows of one device at most 10 rows go to one training shard; that most is reached for some shard in every group.
All inputs are finite; a program needn't handle non-finite values.
Results may differ from a plain program's by a relative error of at most 0.025.
Values may be sent and summed in bfloat16 or wider, within the bound.
A program may use at most 128 MiB of HBM per device.

v0:
```python
import jax
import jax.numpy as jnp
from jax import lax
from jax.sharding import PartitionSpec as P

HEAD_DIM = 128
STEPS = 2


def norm_rows(values, gain):
    wide = values.astype(jnp.float32)
    meansq = jnp.mean(wide * wide, axis=-1, keepdims=True)
    return (wide * lax.rsqrt(meansq + 1e-06) * gain).astype(jnp.bfloat16)


def rounded(values):
    return lax.optimization_barrier(values.astype(jnp.bfloat16)).astype(jnp.float32)


def decode_attend(query, cache_k, cache_v, lengths, new_k, new_v):
    rows_n = query.shape[0]
    slots = cache_k.shape[1]
    kv_n = cache_k.shape[2] // HEAD_DIM
    per_kv = query.shape[1] // cache_k.shape[2]
    scale = 1.0 / HEAD_DIM**0.5
    quer = query.reshape(rows_n, kv_n, per_kv, HEAD_DIM)
    keys_c = cache_k.reshape(rows_n, slots, kv_n, HEAD_DIM)
    vals_c = cache_v.reshape(rows_n, slots, kv_n, HEAD_DIM)
    keys_n = new_k.reshape(rows_n, -1, kv_n, HEAD_DIM)
    vals_n = new_v.reshape(rows_n, -1, kv_n, HEAD_DIM)
    score_c = (
        jnp.einsum("rkgd,rckd->rkgc", quer, keys_c, preferred_element_type=jnp.float32) * scale
    )
    score_n = (
        jnp.einsum("rkgd,rnkd->rkgn", quer, keys_n, preferred_element_type=jnp.float32) * scale
    )
    live = (jnp.arange(slots, dtype=jnp.int32)[None, :] < lengths[:, None])[:, None, None, :]
    score_c = jnp.where(live, score_c, -1e30)
    scores = jnp.concatenate([score_c, score_n], axis=-1)
    expo = jnp.exp(scores)
    weights = (expo / jnp.sum(expo, axis=-1, keepdims=True)).astype(jnp.bfloat16)
    context = jnp.einsum(
        "rkgc,rckd->rkgd", weights[..., :slots], vals_c, preferred_element_type=jnp.float32
    )
    context = context + jnp.einsum(
        "rkgn,rnkd->rkgd", weights[..., slots:], vals_n, preferred_element_type=jnp.float32
    )
    return context.reshape(rows_n, -1).astype(jnp.bfloat16)


def attend(query, keys, values, counts):
    rows_n = counts.shape[0]
    tokens = query.shape[0]
    length = tokens // rows_n
    kv_n = keys.shape[1] // HEAD_DIM
    per_kv = query.shape[1] // keys.shape[1]
    scale = 1.0 / HEAD_DIM**0.5
    quer = query.reshape(rows_n, length, kv_n, per_kv, HEAD_DIM).astype(jnp.float32)
    keyf = keys.reshape(rows_n, length, kv_n, HEAD_DIM).astype(jnp.float32)
    valf = values.reshape(rows_n, length, kv_n, HEAD_DIM).astype(jnp.float32)
    scores = jnp.einsum("rikgd,rjkd->rkgij", quer, keyf) * scale
    slot = jnp.arange(length, dtype=jnp.int32)
    causal = (slot[None, :] <= slot[:, None])[None, :, :]
    inside = slot[None, None, :] < counts[:, None, None]
    mask = (causal & inside)[:, None, None, :, :]
    scores = jnp.where(mask, scores, -1e30)
    expo = jnp.exp(scores)
    weights = (
        (expo / jnp.sum(expo, axis=-1, keepdims=True)).astype(jnp.bfloat16).astype(jnp.float32)
    )
    context = jnp.einsum("rkgij,rjkd->rikgd", weights, valf)
    return context.reshape(tokens, -1).astype(jnp.bfloat16)


def slot_valid(counts, length):
    slot = jnp.arange(length, dtype=jnp.int32)
    return (slot[None, :] < counts[:, None]).reshape(-1)


def exclusive_rank(labels, classes):
    onehot = (labels[:, None] == jnp.arange(classes, dtype=jnp.int32)[None, :]).astype(jnp.int32)
    return jnp.sum((jnp.cumsum(onehot, axis=0) - onehot) * onehot, axis=1)


def on_device(
    hidden_last,
    gain,
    w_query,
    w_key,
    w_value,
    w_out,
    cache_keys,
    cache_values,
    cache_lengths,
    reward_vec,
    response_counts,
    assignment,
    responses,
    cotangent,
):
    query_full, key_full, value_full = (
        lax.all_gather(w_query, "dp", axis=0, tiled=True),
        lax.all_gather(w_key, "dp", axis=0, tiled=True),
        lax.all_gather(w_value, "dp", axis=0, tiled=True),
    )
    state = hidden_last
    keys_new = []
    values_new = []
    for step in range(STEPS):
        normed = norm_rows(state, gain)
        query = jnp.dot(normed, query_full, preferred_element_type=jnp.float32).astype(jnp.bfloat16)
        keys_new.append(
            jnp.dot(normed, key_full, preferred_element_type=jnp.float32).astype(jnp.bfloat16)
        )
        values_new.append(
            jnp.dot(normed, value_full, preferred_element_type=jnp.float32).astype(jnp.bfloat16)
        )
        context = decode_attend(
            query,
            cache_keys,
            cache_values,
            cache_lengths,
            jnp.stack(keys_new, 1),
            jnp.stack(values_new, 1),
        )
        partial_out = jnp.dot(context, w_out, preferred_element_type=jnp.float32)
        state = (
            state.astype(jnp.float32)
            + lax.psum(partial_out.astype(jnp.bfloat16), "tp").astype(jnp.float32)
        ).astype(jnp.bfloat16)
    reward = jnp.sum(state.astype(jnp.float32) * reward_vec, axis=-1)
    total, squares = lax.psum((jnp.sum(reward), jnp.sum(reward * reward)), "dp")
    shards = lax.axis_size("dp")
    rows_dev = reward.shape[0]
    members = rows_dev * shards
    mean = total / members
    spread = squares / members - mean * mean
    advantage = (reward - mean) / jnp.sqrt(spread + 1e-05)
    adv_short = advantage.astype(jnp.bfloat16)
    myself = lax.axis_index("dp")
    group_rows = assignment.shape[0]
    positions = jnp.arange(group_rows, dtype=jnp.int32)
    owner_rank = exclusive_rank(assignment, shards)
    wanted = (assignment[None, :] == myself) & (
        owner_rank[None, :] == jnp.arange(rows_dev, dtype=jnp.int32)[:, None]
    )
    chosen = jnp.sum(jnp.where(wanted, positions[None, :], 0), axis=1)
    every_row, every_adv = (
        lax.all_gather(responses, "dp", axis=0, tiled=True),
        lax.all_gather(adv_short, "dp", axis=0, tiled=True),
    )
    mine = jnp.take(every_row, chosen, axis=0)
    my_adv = jnp.take(every_adv, chosen)
    length = mine.shape[1]
    tokens = mine.shape[0] * length
    local_in = mine.reshape(tokens, -1)
    local_cot = cotangent.reshape(tokens, -1)
    full_in, full_cot = (
        lax.all_gather(local_in, "tp", axis=1, tiled=True),
        lax.all_gather(local_cot, "tp", axis=1, tiled=True),
    )
    normed = norm_rows(full_in, gain)
    query = jnp.dot(normed, query_full, preferred_element_type=jnp.float32).astype(jnp.bfloat16)
    keys = jnp.dot(normed, key_full, preferred_element_type=jnp.float32).astype(jnp.bfloat16)
    values = jnp.dot(normed, value_full, preferred_element_type=jnp.float32).astype(jnp.bfloat16)
    counts = jnp.take(response_counts, chosen)
    valid = slot_valid(counts, length)
    context, pull = jax.vjp(lambda a, b, c: attend(a, b, c, counts), query, keys, values)
    partial_out = jnp.dot(context, w_out, preferred_element_type=jnp.float32)
    layer = (
        local_in.astype(jnp.float32)
        + lax.psum_scatter(
            partial_out.astype(jnp.bfloat16), "tp", scatter_dimension=1, tiled=True
        ).astype(jnp.float32)
    ).astype(jnp.bfloat16)
    token_weight = jnp.repeat(my_adv.astype(jnp.float32), length) * valid.astype(jnp.float32)
    upstream = (token_weight[:, None] * full_cot.astype(jnp.float32)).astype(jnp.bfloat16)
    d_context = lax.dot_general(
        upstream, w_out, (((1,), (1,)), ((), ())), preferred_element_type=jnp.float32
    ).astype(jnp.bfloat16)
    d_query, d_key, d_value = pull(d_context)
    block_rows = lax.all_to_all(normed, "dp", split_axis=1, concat_axis=0, tiled=True)
    width = block_rows.shape[1]
    empty_q = jnp.zeros((width, d_query.shape[1]), jnp.float32)
    empty_k = jnp.zeros((width, d_key.shape[1]), jnp.float32)
    empty_v = jnp.zeros((width, d_value.shape[1]), jnp.float32)
    pieces = (
        lax.all_gather(d_query, "dp", axis=0, tiled=True),
        lax.all_gather(d_key, "dp", axis=0, tiled=True),
        lax.all_gather(d_value, "dp", axis=0, tiled=True),
    )
    span = pieces[0].shape[0]
    count = span // tokens
    totals = list((empty_q, empty_k, empty_v))
    for member in range(count):
        left = block_rows[member * tokens : (member + 1) * tokens]
        for which in range(3):
            right = pieces[which][member * tokens : (member + 1) * tokens]
            term = lax.dot_general(
                left, right, (((0,), (0,)), ((), ())), preferred_element_type=jnp.float32
            )
            totals[which] = totals[which] + rounded(term)
    shard_q, shard_k, shard_v = tuple(totals)
    grad_q, grad_k, grad_v = (
        lax.psum(shard_q.astype(jnp.bfloat16), "grp").astype(jnp.float32),
        lax.psum(shard_k.astype(jnp.bfloat16), "grp").astype(jnp.float32),
        lax.psum(shard_v.astype(jnp.bfloat16), "grp").astype(jnp.float32),
    )
    return (state, advantage, layer.reshape(mine.shape[0], length, -1), grad_q, grad_k, grad_v)


def solution(mesh):
    return jax.shard_map(
        on_device,
        mesh=mesh,
        in_specs=(
            P(("grp", "dp"), None),
            P(),
            P("dp", "tp"),
            P("dp", "tp"),
            P("dp", "tp"),
            P("tp", None),
            P(("grp", "dp"), None, "tp"),
            P(("grp", "dp"), None, "tp"),
            P(("grp", "dp")),
            P(),
            P("grp"),
            P("grp"),
            P(("grp", "dp"), None, "tp"),
            P(("grp", "dp"), None, "tp"),
        ),
        out_specs=(
            P(("grp", "dp"), None),
            P(("grp", "dp")),
            P(("grp", "dp"), None, "tp"),
            P("dp", "tp"),
            P("dp", "tp"),
            P("dp", "tp"),
        ),
        check_vma=False,
    )
```

profile of v0, /device:TPU:0, one launch (start us, length us, event | category | flops | bytes accessed | tf_op | source)
XLA Modules:
  0.0 569.9 jit_solution(5665463674847834380)
XLA Ops:
  7.3 0.7 all-gather.9.cloned.1.call-update
  8.0 0.7 all-gather.11.cloned.1.call-update
  8.7 0.7 all-gather.7.cloned.1.call-update
  9.7 26.9 %all-gather.9.cloned.1.call-done = bf16[5120,128]{1,0:T(8,128)(2,1)} async-done(((bf16[2560,128]{1,0:T(8,128)(2,1)}), bf16[5120,128]{1,0:T(8,128)(2,1)}) %all-gather.9.cloned.1.call-update) | async-done | bytes 1310736 | tf_op jit(solution)/shard_map/all_gather | solution.py:103
  36.6 1.6 convolution_convert_fusion.20
  38.2 24.2 %all-gather.11.cloned.1.call-done = bf16[5120,128]{1,0:T(8,128)(2,1)} async-done(((bf16[2560,128]{1,0:T(8,128)(2,1)}), bf16[5120,128]{1,0:T(8,128)(2,1)}) %all-gather.11.cloned.1.call-update) | async-done | bytes 1310736 | tf_op jit(solution)/shard_map/all_gather | solution.py:104
  62.4 1.6 fusion.68
  64.0 83.2 %all-gather.7.cloned.1.call-done = bf16[5120,640]{1,0:T(8,128)(2,1)} async-done(((bf16[2560,640]{1,0:T(8,128)(2,1)}), bf16[5120,640]{1,0:T(8,128)(2,1)}) %all-gather.7.cloned.1.call-update) | async-done | bytes 6553616 | tf_op jit(solution)/shard_map/all_gather | solution.py:102
  147.2 3.8 convolution_convert_fusion.16
  152.7 4.5 convolution_convert_fusion.2
  157.3 0.5 all-gather.13.cloned.1.call-update
  158.4 0.6 dynamic-slice
  159.6 29.7 %all-reduce.7.cloned.1.call-done = bf16[16,5120]{1,0:T(8,128)(2,1)} async-done(((bf16[16,5120]{1,0:T(8,128)(2,1)}), bf16[16,5120]{1,0:T(8,128)(2,1)}) %all-reduce.7.cloned.1.call-update) | async-done | bytes 163856 | tf_op jit(solution)/shard_map/psum | solution.py:129
  189.3 1.1 fusion.26
  190.4 1.0 fusion.28
  191.4 4.5 convolution_convert_fusion.15
  196.0 0.9 reshape.456
  196.8 1.0 fusion.71
  198.4 1.0 copy.123
  200.7 4.5 convolution_convert_fusion.1
  205.3 9.6 %all-gather.13.cloned.1.call-done = bf16[32,16,1280]{2,1,0:T(8,128)(2,1)} async-done(((bf16[16,16,1280]{2,1,0:T(8,128)(2,1)}), bf16[32,16,1280]{2,1,0:T(8,128)(2,1)}) %all-gather.13.cloned.1.call-update) | async-done | bytes 1310736 | tf_op jit(solution)/shard_map/all_gather | solution.py:149
  215.0 1.9 gather_fusion
  216.9 32.8 %all-reduce.9.cloned.1.call-done = bf16[16,5120]{1,0:T(8,128)(2,1)} async-done(((bf16[16,5120]{1,0:T(8,128)(2,1)}), bf16[16,5120]{1,0:T(8,128)(2,1)}) %all-reduce.9.cloned.1.call-update) | async-done | bytes 163856 | tf_op jit(solution)/shard_map/psum | solution.py:129
  249.7 2.3 fusion.36
  251.9 0.6 multiply_reduce_fusion
  252.5 5.5 all-reduce.1
  260.7 0.5 fusion.66
  261.4 4.9 all-reduce
  266.3 0.7 gather_fusion.2
  267.2 1.0 bitcast_select_fusion
  268.3 0.7 all-gather.17.cloned.1.call-update
  269.2 0.7 gather_fusion.1
  270.2 23.7 %all-gather.15.cloned.1.call-done = bf16[256,5120]{1,0:T(8,128)(2,1)} async-done(((bf16[256,1280]{1,0:T(8,128)(2,1)}), bf16[256,5120]{1,0:T(8,128)(2,1)}) %all-gather.15.cloned.1.call-update) | async-done | bytes 2621456 | tf_op jit(solution)/shard_map/all_gather | solution.py:159
  293.9 2.5 fusion
  296.4 0.8 fusion.2
  297.2 5.1 convolution_convert_fusion.11
  302.7 2.7 convolution_convert_fusion.13
  305.4 0.8 fusion.69
  306.2 0.8 convolution_convert_fusion.14
  307.5 6.6 %convolution_convert_fusion = bf16[256,5120]{1,0:T(8,128)(2,1)} fusion(bf16[640,5120]{1,0:T(8,128)(2,1)} %param.19, bf16[32,8,5,128]{3,2,1,0:T(8,128)(2,1)S(1)} %bitcast.188), kind=kOutput, calls=%fused_computation.6 | convolution fusion | flops 1679032320 | bytes 9502720 | tf_op jit(solution)/shard_map/dot_general | solution.py:169
  314.2 6.9 %all-gather.17.cloned.1.call-done = bf16[256,5120]{1,0:T(8,128)(2,1)} async-done(((bf16[256,1280]{1,0:T(8,128)(2,1)}), bf16[256,5120]{1,0:T(8,128)(2,1)}) %all-gather.17.cloned.1.call-update) | async-done | bytes 2621456 | tf_op jit(solution)/shard_map/all_gather | solution.py:160
  321.0 5.9 %fusion.6 = bf16[256,640]{1,0:T(8,128)(2,1)S(1)} fusion(bf16[640,5120]{1,0:T(8,128)(2,1)} %param.19, bf16[256,5120]{1,0:T(8,128)(2,1)} %all-gather.17.cloned.1.call-done, f32[256]{0:T(256)S(1)} %mul.176), kind=kOutput, calls=%fused_computation.29 | convolution fusion | flops 1681817600 | bytes 9503744 | tf_op jit(solution)/shard_map/dot_general | solution.py:178
  326.9 0.4 reshape.465
  327.3 1.7 copy.184
  329.0 4.2 all-to-all-start
  333.5 1.9 fusion.21
  335.5 1.5 convolution_convert_fusion.12
  337.6 28.2 %all_gather.38 = bf16[512,128]{1,0:T(8,128)(2,1)S(1)} all-gather(bf16[256,128]{1,0:T(8,128)(2,1)S(1)} %bitcast.195), channel_id=1, replica_groups=mesh['grp'=4,'dp'=2,'tp'=4] {'dp'}, dimensions={0}, use_global_device_ids=true | all-gather | bytes 196608 | tf_op jit(solution)/shard_map/all_gather | solution.py:189
  366.1 4.9 all_gather.39
  371.0 8.6 %all_gather.37 = bf16[512,640]{1,0:T(8,128)(2,1)} all-gather(bf16[256,640]{1,0:T(8,128)(2,1)S(1)} %bitcast.185), channel_id=1, replica_groups=mesh['grp'=4,'dp'=2,'tp'=4] {'dp'}, dimensions={0}, use_global_device_ids=true | all-gather | bytes 983040 | tf_op jit(solution)/shard_map/all_gather | solution.py:188
  379.6 0.6 convolution_convert_fusion.8
  380.2 0.6 convolution_convert_fusion.7
  380.8 0.6 convolution_convert_fusion.6
  381.3 0.6 convolution_convert_fusion.5
  381.9 1.2 convolution_convert_fusion.4
  383.1 1.2 convolution_convert_fusion.3
  384.4 1.5 add_convert_fusion.1
  385.8 2.6 add_convert_fusion
  388.5 1.0 copy-done.9
  389.5 2.2 add_convert_fusion.3
  391.7 163.8 %all-reduce.11.cloned.1.call-done = (bf16[2560,640]{1,0:T(8,128)(2,1)}, bf16[2560,128]{1,0:T(8,128)(2,1)}, bf16[2560,128]{1,0:T(8,128)(2,1)}) async-done(((bf16[2560,640]{1,0:T(8,128)(2,1)}, bf16[2560,128]{1,0:T(8,128)(2,1)}, bf16[2560,128]{1,0:T(8,128)(2,1)}), (bf16[2560,640]{1,0:T(8,128)(2,1)}, bf16[2560,128]{1,0:T(8,128)(2,1)}, bf16[2560,128]{1,0:T(8,128)(2,1)})) %all-reduce.11.cloned.1.call-update) | async-done | bytes 4587536 | tf_op jit(solution)/shard_map/psum | solution.py:205
  555.5 5.3 convert_element_type.283
  560.8 1.1 convert_element_type.290
  561.9 1.1 convert_element_type.299
  (149 shorter events, 7.4 us)
Async XLA Ops:
  7.2 144.2 %copy-start = (bf16[16,128,128]{2,1,0:T(8,128)(2,1)S(1)}, bf16[16,128,128]{2,1,0:T(8,128)(2,1)}, u32[]{:S(2)}) copy-start(bf16[16,128,128]{2,1,0:T(8,128)(2,1)} %param.20) | copy-start | bytes 1572868
  7.2 2.3 copy-start.7
  7.2 2.5 copy-start.31
  7.2 29.3 %copy-start.22 = (f32[5120]{0:T(1024)S(1)}, f32[5120]{0:T(1024)}, u32[]{:S(2)}) copy-start(f32[5120]{0:T(1024)} %param.15) | copy-start | bytes 61444
  7.2 29.3 %all-gather.9.cloned.1.call-start = ((), (), s32[]{:S(2)}) async-start(), calls=%async_computation.3 | async-start | bytes 1966080 | tf_op jit(solution)/shard_map/all_gather | solution.py:103
  7.9 54.4 %all-gather.11.cloned.1.call-start = ((), (), s32[]{:S(2)}) async-start(), calls=%async_computation.4 | async-start | bytes 1966080 | tf_op jit(solution)/shard_map/all_gather | solution.py:104
  8.7 138.5 %all-gather.7.cloned.1.call-start = ((), (), s32[]{:S(2)}) async-start(), calls=%async_computation.2 | async-start | bytes 9830400 | tf_op jit(solution)/shard_map/all_gather | solution.py:102
  9.4 179.9 %all-reduce.7.cloned.1.call-start = ((), (), s32[]{:S(2)}) async-start(), calls=%async_computation.5 | async-start | bytes 327680 | tf_op jit(solution)/shard_map/psum | solution.py:129
  151.1 1.3 copy-start.11
  152.7 5.2 copy-start.30
  152.7 5.7 copy-start.34
  157.2 57.7 %all-gather.13.cloned.1.call-start = ((), (), s32[]{:S(2)}) async-start(), calls=%async_computation.7 | async-start | bytes 1966080 | tf_op jit(solution)/shard_map/all_gather | solution.py:149
  157.8 91.8 %all-reduce.9.cloned.1.call-start = ((), (), s32[]{:S(2)}) async-start(), calls=%async_computation.6 | async-start | bytes 327680 | tf_op jit(solution)/shard_map/psum | solution.py:129
  158.3 31.0 %copy-start.32 = (s32[16]{0:T(128)}, s32[16]{0:T(128)S(1)}, u32[]{:S(2)}) copy-start(s32[16]{0:T(128)S(1)} %select_reduce_fusion.1) | copy-start | bytes 196
  191.4 6.4 %copy-start.3 = (bf16[5120,128]{1,0:T(8,128)(2,1)S(1)}, bf16[5120,128]{1,0:T(8,128)(2,1)}, u32[]{:S(2)}) copy-start(bf16[5120,128]{1,0:T(8,128)(2,1)} %all-gather.9.cloned.1.call-done) | copy-start | bytes 3932164
  196.0 4.0 copy-start.4
  198.1 2.1 copy-start.12
  200.7 49.0 %copy-start.13 = (bf16[16,5120]{1,0:T(8,128)(2,1)S(1)}, bf16[16,5120]{1,0:T(8,128)(2,1)}, u32[]{:S(2)}) copy-start(bf16[16,5120]{1,0:T(8,128)(2,1)} %all-reduce.7.cloned.1.call-done) | copy-start | bytes 491524
  200.7 49.0 %copy-start.29 = (f32[5120]{0:T(1024)S(1)}, f32[5120]{0:T(1024)}, u32[]{:S(2)}) copy-start(f32[5120]{0:T(1024)} %param.23) | copy-start | bytes 61444
  205.2 61.8 %copy-start.33 = (s32[16]{0:T(128)S(1)}, s32[16]{0:T(128)}, u32[]{:S(2)}) copy-start(s32[16]{0:T(128)} %copy-done.32) | copy-start | bytes 196
  205.3 63.9 %copy-start.2 = (s32[32]{0:T(128)S(1)}, s32[32]{0:T(128)}, u32[]{:S(2)}) copy-start(s32[32]{0:T(128)} %param.24) | copy-start | bytes 388
  205.3 88.6 %all-gather.15.cloned.1.call-start = ((), (), s32[]{:S(2)}) async-start(), calls=%async_computation.8 | async-start | bytes 3276800 | tf_op jit(solution)/shard_map/all_gather | solution.py:159
  216.9 79.5 %copy-start.8 = (bf16[16,16,1280]{2,1,0:T(8,128)(2,1)}, bf16[16,16,1280]{2,1,0:T(8,128)(2,1)S(1)}, u32[]{:S(2)}) copy-start(bf16[16,16,1280]{2,1,0:T(8,128)(2,1)S(1)} %gather_fusion) | copy-start | bytes 1966084
  268.2 52.8 %all-gather.17.cloned.1.call-start = ((), (), s32[]{:S(2)}) async-start(), calls=%async_computation.10 | async-start | bytes 3276800 | tf_op jit(solution)/shard_map/all_gather | solution.py:160
  269.0 119.5 %reduce-scatter.2.cloned.1.call-start = ((), (), s32[]{:S(2)}) async-start(), calls=%async_computation.9 | async-start | bytes 3276800 | tf_op jit(solution)/shard_map/reduce_scatter | solution.py:172
  270.2 35.1 %copy-start.27 = (pred[16,16,16]{1,2,0:T(8,128)(4,1)}, pred[16,16,16]{1,2,0:T(8,128)(4,1)S(1)}, u32[]{:S(2)}) copy-start(pred[16,16,16]{1,2,0:T(8,128)(4,1)S(1)} %broadcast_and_fusion) | copy-start | bytes 12292
  293.9 2.5 copy-start.6
  302.7 4.4 copy-start.20
  302.7 3.5 copy-start.5
  305.3 2.0 copy-start.23
  306.2 1.2 copy-start.16
  306.2 1.2 copy-start.25
  327.3 6.2 %copy-start.14 = (bf16[16,16,1,5,128]{4,3,1,0,2:T(8,128)(2,1)}, bf16[16,16,1,5,128]{4,3,1,0,2:T(8,128)(2,1)S(1)}, u32[]{:S(2)}) copy-start(bf16[16,16,1,5,128]{4,3,1,0,2:T(8,128)(2,1)S(1)} %reshape.465) | copy-start | bytes 983044
  329.0 4.5 copy-start.26
  329.0 6.4 %copy-start.24 = (bf16[256,128]{1,0:T(8,128)(2,1)S(1)}, bf16[256,128]{1,0:T(8,128)(2,1)}, u32[]{:S(2)}) copy-start(bf16[256,128]{1,0:T(8,128)(2,1)} %copy-done.23) | copy-start | bytes 196612
  329.0 6.4 %copy-start.28 = (pred[16,16,16]{1,2,0:T(8,128)(4,1)S(1)}, pred[16,16,16]{1,2,0:T(8,128)(4,1)}, u32[]{:S(2)}) copy-start(pred[16,16,16]{1,2,0:T(8,128)(4,1)} %copy-done.27) | copy-start | bytes 12292
  329.0 50.6 %all-to-all-start = ((bf16[256,2,2560]{2,0,1:T(8,128)(2,1)}), bf16[256,2,2560]{2,0,1:T(8,128)(2,1)S(1)}, u32[]{:S(2)}, u32[]{:S(2)}) async-start(bf16[256,2,2560]{2,0,1:T(8,128)(2,1)} %bitcast.181), calls=%async_computation.1 | async-start | bytes 5242880 | tf_op jit(solution)/shard_map/all_to_all | solution.py:182
  333.2 222.3 %all-reduce.11.cloned.1.call-start = ((), (), s32[]{:S(2)}) async-start(), calls=%async_computation.11 | async-start | bytes 9175040 | tf_op jit(solution)/shard_map/psum | solution.py:205
  335.4 1.8 copy-start.17
  335.4 1.8 copy-start.21
  337.0 28.7 %copy-start.15 = (bf16[16,16,1,5,128]{4,3,1,0,2:T(8,128)(2,1)S(1)}, bf16[16,16,1,5,128]{4,3,1,0,2:T(8,128)(2,1)}, u32[]{:S(2)}) copy-start(bf16[16,16,1,5,128]{4,3,1,0,2:T(8,128)(2,1)} %copy-done.14) | copy-start | bytes 983044
  380.2 1.7 copy-start.10
  388.4 1.1 copy-start.9
  555.5 5.3 copy-start.19
  555.5 6.4 %copy-start.18 = (bf16[2560,128]{1,0:T(8,128)(2,1)S(1)}, bf16[2560,128]{1,0:T(8,128)(2,1)}, u32[]{:S(2)}) copy-start(bf16[2560,128]{1,0:T(8,128)(2,1)} %get-tuple-element.12) | copy-start | bytes 1966084
  555.5 7.6 %copy-start.1 = (bf16[16,128,128]{2,1,0:T(8,128)(2,1)S(1)}, bf16[16,128,128]{2,1,0:T(8,128)(2,1)}, u32[]{:S(2)}) copy-start(bf16[16,128,128]{2,1,0:T(8,128)(2,1)} %param.20) | copy-start | bytes 1572868
Sparse Core Ops, SparseCore 0:
  9.6 26.9 all-gather.8
  38.1 24.2 all-gather.10
  63.9 83.2 all-gather.6
  157.4 31.9 all-reduce.6
  190.7 24.2 all-gather.12
  217.7 31.9 all-reduce.8
  268.3 25.5 all-gather.14
  295.5 25.5 all-gather.16
  323.6 34.3 reduce-scatter.1
  388.6 166.8 all-reduce.10
where the time goes:
time: 571 us; the launch traced here: 570 us
  waiting for transfers between devices  404 us (71%)
  matrix products  54.5 us (10%)
  blocking collectives  52.2 us (9%)
  other arithmetic  24.9 us (4%)
  between operations  18.2 us (3%)
  local copies, waits for them, and re-layouts  11 us (2%)
    psum x1, waiting for transfers between devices, on_device(): lax.psum(shard_q.astype(jnp.bfloat16), 'grp').astype(jnp.float32)  164 us
    all_gather x1, waiting for transfers between devices, on_device(): lax.all_gather(w_query, 'dp', axis=0, tiled=True)  83.2 us
    psum x2, waiting for transfers between devices, on_device(): lax.psum(partial_out.astype(jnp.bfloat16), 'tp').astype(jnp.float32)  62.5 us
    all_gather x1, blocking collectives, on_device(): lax.all_gather(d_key, 'dp', axis=0, tiled=True)  28.2 us
    all_gather x1, waiting for transfers between devices, on_device(): lax.all_gather(w_key, 'dp', axis=0, tiled=True)  26.9 us
    all_gather x1, waiting for transfers between devices, on_device(): lax.all_gather(w_value, 'dp', axis=0, tiled=True)  24.2 us
    all_gather x1, waiting for transfers between devices, on_device(): lax.all_gather(local_in, 'tp', axis=1, tiled=True)  23.7 us
    dot_general x3, matrix products, on_device(): partial_out = jnp.dot(context, w_out, preferred_element_type=jnp.float32)  15.7 us
  transfers between devices with their start and end apart: 11, of which 9 were waited for; matrix products, arithmetic and copies ran while one was open for 12% of the time, Pallas kernels for 0%

commit v1 on v0

--- a/solution.py
+++ b/solution.py
@@ -202,7 +202,7 @@
             totals[which] = totals[which] + rounded(term)
     shard_q, shard_k, shard_v = tuple(totals)
     grad_q, grad_k, grad_v = (
-        lax.psum(shard_q.astype(jnp.bfloat16), "grp").astype(jnp.float32),
+        jnp.sum(lax.all_gather(shard_q.astype(jnp.bfloat16), "grp"), axis=0).astype(jnp.float32),
         lax.psum(shard_k.astype(jnp.bfloat16), "grp").astype(jnp.float32),
         lax.psum(shard_v.astype(jnp.bfloat16), "grp").astype(jnp.float32),
     )

time: 571 us -> 708 us (1.24)
  waiting for transfers between devices: 404 us -> 532 us
  other arithmetic: 24.9 us -> 36.1 us
    all_gather x0 -> x1, waiting for transfers between devices: none -> 227 us  [on_device(): lax.all_gather(shard_q.astype(jnp.bfloat16), 'grp')]
    psum x1, waiting for transfers between devices: 164 us -> 35.1 us  [on_device(): lax.psum(shard_k.astype(jnp.bfloat16), 'grp').astype(jnp.float32)]
    reduce_scatter x1, waiting for transfers between devices: 0.02 us -> 31.9 us  [on_device(): lax.psum_scatter(partial_out.astype(jnp.bfloat16), 'tp', scatter_dimensio...]
    all_gather x1, blocking collectives: 28.2 us -> 4.94 us  [on_device(): lax.all_gather(d_key, 'dp', axis=0, tiled=True)]
    all_gather x1, blocking collectives: 4.94 us -> 21.1 us  [on_device(): lax.all_gather(d_value, 'dp', axis=0, tiled=True)]
    reduce_sum x0 -> x1, other arithmetic: none -> 9.24 us  [on_device(): jnp.sum(lax.all_gather(shard_q.astype(jnp.bfloat16), 'grp'), axis=0)]
    dot_general x6, matrix products: 4.68 us -> 12.6 us  [on_device(): lax.dot_general(left, right, (((0,), (0,)), ((), ())), preferred_element_...]
  transfers between devices with their start and end apart: 11 -> 12, of which waited for: 9 -> 11; matrix products, arithmetic and copies ran while one was open for 12% -> 10% of each run, Pallas kernels for 0% -> 0%
where the time goes in v1:
time: 708 us; the launch traced here: 707 us
  waiting for transfers between devices  532 us (75%)
  matrix products  59.7 us (8%)
  blocking collectives  45.3 us (6%)
  other arithmetic  36.1 us (5%)
  between operations  17.7 us (2%)
  local copies, waits for them, and re-layouts  10.7 us (2%)
    all_gather x1, waiting for transfers between devices, on_device(): lax.all_gather(shard_q.astype(jnp.bfloat16), 'grp')  227 us
    all_gather x1, waiting for transfers between devices, on_device(): lax.all_gather(w_query, 'dp', axis=0, tiled=True)  83.2 us
    psum x2, waiting for transfers between devices, on_device(): lax.psum(partial_out.astype(jnp.bfloat16), 'tp').astype(jnp.float32)  64.2 us
    psum x1, waiting for transfers between devices, on_device(): lax.psum(shard_k.astype(jnp.bfloat16), 'grp').astype(jnp.float32)  35.1 us
    reduce_scatter x1, waiting for transfers between devices, on_device(): lax.psum_scatter(partial_out.astype(jnp.bfloat16), 'tp', scatter_dimensio...  31.9 us
    all_gather x1, waiting for transfers between devices, on_device(): lax.all_gather(w_key, 'dp', axis=0, tiled=True)  26.9 us
    all_gather x1, waiting for transfers between devices, on_device(): lax.all_gather(w_value, 'dp', axis=0, tiled=True)  24.2 us
    all_gather x1, waiting for transfers between devices, on_device(): lax.all_gather(local_in, 'tp', axis=1, tiled=True)  21.2 us
  transfers between devices with their start and end apart: 12, of which 11 were waited for; matrix products, arithmetic and copies ran while one was open for 10% of the time, Pallas kernels for 0%

profile of v1, /device:TPU:0, one launch (start us, length us, event | category | flops | bytes accessed | tf_op | source)
XLA Modules:
  0.0 706.9 jit_solution(10655818466756849814)
XLA Ops:
  7.3 0.7 all-gather.11.cloned.1.call-update
  8.0 0.7 all-gather.13.cloned.1.call-update
  8.7 0.7 all-gather.9.cloned.1.call-update
  9.7 26.9 %all-gather.11.cloned.1.call-done = bf16[5120,128]{1,0:T(8,128)(2,1)} async-done(((bf16[2560,128]{1,0:T(8,128)(2,1)}), bf16[5120,128]{1,0:T(8,128)(2,1)}) %all-gather.11.cloned.1.call-update) | async-done | bytes 1310736 | tf_op jit(solution)/shard_map/all_gather | solution.py:103
  36.6 1.6 convolution_convert_fusion.20
  38.2 24.2 %all-gather.13.cloned.1.call-done = bf16[5120,128]{1,0:T(8,128)(2,1)} async-done(((bf16[2560,128]{1,0:T(8,128)(2,1)}), bf16[5120,128]{1,0:T(8,128)(2,1)}) %all-gather.13.cloned.1.call-update) | async-done | bytes 1310736 | tf_op jit(solution)/shard_map/all_gather | solution.py:104
  62.4 1.6 fusion.68
  64.0 83.2 %all-gather.9.cloned.1.call-done = bf16[5120,640]{1,0:T(8,128)(2,1)} async-done(((bf16[2560,640]{1,0:T(8,128)(2,1)}), bf16[5120,640]{1,0:T(8,128)(2,1)}) %all-gather.9.cloned.1.call-update) | async-done | bytes 6553616 | tf_op jit(solution)/shard_map/all_gather | solution.py:102
  147.2 3.8 convolution_convert_fusion.16
  152.7 4.5 convolution_convert_fusion.2
  157.2 0.5 all-gather.15.cloned.1.call-update
  157.8 31.4 %all-reduce.7.cloned.1.call-done = bf16[16,5120]{1,0:T(8,128)(2,1)} async-done(((bf16[16,5120]{1,0:T(8,128)(2,1)}), bf16[16,5120]{1,0:T(8,128)(2,1)}) %all-reduce.7.cloned.1.call-update) | async-done | bytes 163856 | tf_op jit(solution)/shard_map/psum | solution.py:129
  189.3 1.1 fusion.26
  190.4 1.0 fusion.28
  191.4 4.5 convolution_convert_fusion.15
  195.9 0.9 reshape.456
  196.8 1.0 fusion.71
  198.4 1.0 copy.123
  200.7 4.5 convolution_convert_fusion.1
  205.3 0.7 all-gather.19.cloned.1.call-update
  206.1 0.6 dynamic-slice
  207.8 7.1 %all-gather.15.cloned.1.call-done = bf16[32,16,1280]{2,1,0:T(8,128)(2,1)} async-done(((bf16[16,16,1280]{2,1,0:T(8,128)(2,1)}), bf16[32,16,1280]{2,1,0:T(8,128)(2,1)}) %all-gather.15.cloned.1.call-update) | async-done | bytes 1310736 | tf_op jit(solution)/shard_map/all_gather | solution.py:149
  214.9 1.9 gather_fusion
  216.8 32.8 %all-reduce.9.cloned.1.call-done = bf16[16,5120]{1,0:T(8,128)(2,1)} async-done(((bf16[16,5120]{1,0:T(8,128)(2,1)}), bf16[16,5120]{1,0:T(8,128)(2,1)}) %all-reduce.9.cloned.1.call-update) | async-done | bytes 163856 | tf_op jit(solution)/shard_map/psum | solution.py:129
  249.6 2.3 fusion.36
  251.9 0.6 multiply_reduce_fusion
  252.5 5.5 all-reduce.1
  261.4 4.9 all-reduce
  266.3 0.7 gather_fusion.2
  267.2 1.0 bitcast_select_fusion
  268.2 0.7 gather_fusion.1
  269.0 7.7 %all-gather.19.cloned.1.call-done = bf16[256,5120]{1,0:T(8,128)(2,1)} async-done(((bf16[256,1280]{1,0:T(8,128)(2,1)}), bf16[256,5120]{1,0:T(8,128)(2,1)}) %all-gather.19.cloned.1.call-update) | async-done | bytes 2621456 | tf_op jit(solution)/shard_map/all_gather | solution.py:160
  276.8 5.9 fusion.6
  283.2 21.2 %all-gather.17.cloned.1.call-done = bf16[256,5120]{1,0:T(8,128)(2,1)} async-done(((bf16[256,1280]{1,0:T(8,128)(2,1)}), bf16[256,5120]{1,0:T(8,128)(2,1)}) %all-gather.17.cloned.1.call-update) | async-done | bytes 2621456 | tf_op jit(solution)/shard_map/all_gather | solution.py:159
  304.5 2.5 fusion
  307.0 0.8 fusion.2
  307.8 1.7 copy.184
  309.4 5.2 all-to-all-start
  314.7 5.1 convolution_convert_fusion.11
  319.7 1.2 reshape.461
  320.9 2.3 convolution_convert_fusion.13
  323.2 0.8 fusion.69
  324.0 0.8 convolution_convert_fusion.14
  324.9 0.8 fusion.21
  326.0 21.1 %all_gather.47 = bf16[512,128]{1,0:T(8,128)(2,1)S(1)} all-gather(bf16[256,128]{1,0:T(8,128)(2,1)S(1)} %bitcast.191), channel_id=1, replica_groups=mesh['grp'=4,'dp'=2,'tp'=4] {'dp'}, dimensions={0}, use_global_device_ids=true | all-gather | bytes 196608 | tf_op jit(solution)/shard_map/all_gather | solution.py:190
  347.5 4.9 all_gather.46
  352.4 1.9 convolution_convert_fusion.7
  354.3 1.9 convolution_convert_fusion.8
  356.2 1.9 convolution_convert_fusion.5
  358.0 1.9 convolution_convert_fusion.6
  359.9 1.4 add_convert_fusion.1
  361.9 6.5 convolution_convert_fusion
  369.0 8.8 %all_gather.43 = bf16[512,640]{1,0:T(8,128)(2,1)S(1)} all-gather(bf16[256,640]{1,0:T(8,128)(2,1)S(1)} %bitcast.181), channel_id=1, replica_groups=mesh['grp'=4,'dp'=2,'tp'=4] {'dp'}, dimensions={0}, use_global_device_ids=true | all-gather | bytes 983040 | tf_op jit(solution)/shard_map/all_gather | solution.py:188
  377.9 2.5 convolution_convert_fusion.4
  380.4 2.6 convolution_convert_fusion.3
  383.0 2.6 add_convert_fusion
  385.6 35.1 %all-reduce.11.cloned.1.call-done = (bf16[2560,128]{1,0:T(8,128)(2,1)}, bf16[2560,128]{1,0:T(8,128)(2,1)}) async-done(((bf16[2560,128]{1,0:T(8,128)(2,1)}, bf16[2560,128]{1,0:T(8,128)(2,1)}), (bf16[2560,128]{1,0:T(8,128)(2,1)}, bf16[2560,128]{1,0:T(8,128)(2,1)})) %all-reduce.11.cloned.1.call-update) | async-done | bytes 1310736 | tf_op jit(solution)/shard_map/psum | solution.py:206
  420.7 2.2 convert_element_type.292
  422.9 2.2 convert_element_type.301
  425.2 31.9 %reduce-scatter.2.cloned.1.call-done = bf16[256,1280]{1,0:T(8,128)(2,1)} async-done(((bf16[256,5120]{1,0:T(8,128)(2,1)}), bf16[256,1280]{1,0:T(8,128)(2,1)}) %reduce-scatter.2.cloned.1.call-update) | async-done | bytes 655376 | tf_op jit(solution)/shard_map/reduce_scatter | solution.py:172
  457.1 2.2 add_convert_fusion.3
  459.3 226.7 %all-gather.21.cloned.1.call-done = bf16[10240,640]{1,0:T(8,128)(2,1)} async-done(((bf16[2560,640]{1,0:T(8,128)(2,1)}), bf16[10240,640]{1,0:T(8,128)(2,1)}) %all-gather.21.cloned.1.call-update) | async-done | bytes 13107216 | tf_op jit(solution)/shard_map/all_gather | solution.py:205
  686.0 9.2 %reduce_sum.139 = bf16[2560,640]{1,0:T(8,128)(2,1)} reduce(bf16[4,2560,640]{2,1,0:T(8,128)(2,1)} %bitcast.176, bf16[]{:T(256)} %constant.84.clone.1), dimensions={0}, to_apply=%region_18.19 | reduce | flops 4915200 | bytes 16384002 | tf_op jit(solution)/shard_map/reduce_sum | solution.py:205
  695.2 5.1 convert_element_type.285
  (125 shorter events, 7.8 us)
Async XLA Ops:
  7.2 144.2 %copy-start = (bf16[16,128,128]{2,1,0:T(8,128)(2,1)S(1)}, bf16[16,128,128]{2,1,0:T(8,128)(2,1)}, u32[]{:S(2)}) copy-start(bf16[16,128,128]{2,1,0:T(8,128)(2,1)} %param.20) | copy-start | bytes 1572868
  7.2 2.3 copy-start.7
  7.2 2.5 copy-start.19
  7.2 29.3 %copy-start.16 = (f32[5120]{0:T(1024)S(1)}, f32[5120]{0:T(1024)}, u32[]{:S(2)}) copy-start(f32[5120]{0:T(1024)} %param.15) | copy-start | bytes 61444
  7.2 29.3 %all-gather.11.cloned.1.call-start = ((), (), s32[]{:S(2)}) async-start(), calls=%async_computation.3 | async-start | bytes 1966080 | tf_op jit(solution)/shard_map/all_gather | solution.py:103
  7.9 54.4 %all-gather.13.cloned.1.call-start = ((), (), s32[]{:S(2)}) async-start(), calls=%async_computation.4 | async-start | bytes 1966080 | tf_op jit(solution)/shard_map/all_gather | solution.py:104
  8.7 138.5 %all-gather.9.cloned.1.call-start = ((), (), s32[]{:S(2)}) async-start(), calls=%async_computation.2 | async-start | bytes 9830400 | tf_op jit(solution)/shard_map/all_gather | solution.py:102
  9.4 179.8 %all-reduce.7.cloned.1.call-start = ((), (), s32[]{:S(2)}) async-start(), calls=%async_computation.5 | async-start | bytes 327680 | tf_op jit(solution)/shard_map/psum | solution.py:129
  151.1 1.3 copy-start.10
  157.2 57.7 %all-gather.15.cloned.1.call-start = ((), (), s32[]{:S(2)}) async-start(), calls=%async_computation.7 | async-start | bytes 1966080 | tf_op jit(solution)/shard_map/all_gather | solution.py:149
  157.8 91.8 %all-reduce.9.cloned.1.call-start = ((), (), s32[]{:S(2)}) async-start(), calls=%async_computation.6 | async-start | bytes 327680 | tf_op jit(solution)/shard_map/psum | solution.py:129
  191.4 6.4 copy-start.3
  195.9 4.0 copy-start.4
  198.1 2.1 copy-start.11
  200.7 5.4 copy-start.20
  200.7 6.7 copy-start.18
  200.7 48.9 %copy-start.12 = (bf16[16,5120]{1,0:T(8,128)(2,1)S(1)}, bf16[16,5120]{1,0:T(8,128)(2,1)}, u32[]{:S(2)}) copy-start(bf16[16,5120]{1,0:T(8,128)(2,1)} %all-reduce.7.cloned.1.call-done) | copy-start | bytes 491524
  200.7 48.9 %copy-start.17 = (f32[5120]{0:T(1024)S(1)}, f32[5120]{0:T(1024)}, u32[]{:S(2)}) copy-start(f32[5120]{0:T(1024)} %param.23) | copy-start | bytes 61444
  205.3 71.5 %all-gather.19.cloned.1.call-start = ((), (), s32[]{:S(2)}) async-start(), calls=%async_computation.10 | async-start | bytes 3276800 | tf_op jit(solution)/shard_map/all_gather | solution.py:160
  205.3 62.9 %copy-start.2 = (s32[32]{0:T(128)S(1)}, s32[32]{0:T(128)}, u32[]{:S(2)}) copy-start(s32[32]{0:T(128)} %param.24) | copy-start | bytes 388
  206.0 98.4 %all-gather.17.cloned.1.call-start = ((), (), s32[]{:S(2)}) async-start(), calls=%async_computation.8 | async-start | bytes 3276800 | tf_op jit(solution)/shard_map/all_gather | solution.py:159
  216.8 65.8 %copy-start.8 = (bf16[16,16,1280]{2,1,0:T(8,128)(2,1)}, bf16[16,16,1280]{2,1,0:T(8,128)(2,1)S(1)}, u32[]{:S(2)}) copy-start(bf16[16,16,1280]{2,1,0:T(8,128)(2,1)S(1)} %gather_fusion) | copy-start | bytes 1966084
  304.5 2.5 copy-start.6
  309.4 43.0 %all-to-all-start = ((bf16[256,2,2560]{2,0,1:T(8,128)(2,1)}), bf16[256,2,2560]{2,0,1:T(8,128)(2,1)}, u32[]{:S(2)}, u32[]{:S(2)}) async-start(bf16[256,2,2560]{2,0,1:T(8,128)(2,1)} %bitcast.177), calls=%async_computation.1 | async-start | bytes 5242880 | tf_op jit(solution)/shard_map/all_to_all | solution.py:182
  314.6 106.1 %all-reduce.11.cloned.1.call-start = ((), (), s32[]{:S(2)}) async-start(), calls=%async_computation.12 | async-start | bytes 2621440 | tf_op jit(solution)/shard_map/psum | solution.py:206
  320.9 2.3 copy-start.15
  320.9 3.1 copy-start.5
  324.0 23.1 %copy-start.13 = (f32[16,1,5,16,16]{3,4,2,0,1:T(8,128)}, f32[16,1,5,16,16]{3,4,2,0,1:T(8,128)S(1)}, u32[]{:S(2)}) copy-start(f32[16,1,5,16,16]{3,4,2,0,1:T(8,128)S(1)} %get-tuple-element.20) | copy-start | bytes 245764
  359.9 1.5 copy-start.14
  361.4 95.7 %reduce-scatter.2.cloned.1.call-start = ((), (), s32[]{:S(2)}) async-start(), calls=%async_computation.9 | async-start | bytes 3276800 | tf_op jit(solution)/shard_map/reduce_scatter | solution.py:172
  368.4 317.6 %all-gather.21.cloned.1.call-start = ((), (), s32[]{:S(2)}) async-start(), calls=%async_computation.11 | async-start | bytes 16384000 | tf_op jit(solution)/shard_map/all_gather | solution.py:205
  385.6 71.5 %copy-start.9 = (bf16[16,16,1280]{2,1,0:T(8,128)(2,1)S(1)}, bf16[16,16,1280]{2,1,0:T(8,128)(2,1)}, u32[]{:S(2)}) copy-start(bf16[16,16,1280]{2,1,0:T(8,128)(2,1)} %copy-done.8) | copy-start | bytes 1966084
  686.0 14.4 %copy-start.1 = (bf16[16,128,128]{2,1,0:T(8,128)(2,1)S(1)}, bf16[16,128,128]{2,1,0:T(8,128)(2,1)}, u32[]{:S(2)}) copy-start(bf16[16,128,128]{2,1,0:T(8,128)(2,1)} %param.20) | copy-start | bytes 1572868
Sparse Core Ops, SparseCore 0:
  9.6 26.9 all-gather.10
  38.1 24.2 all-gather.12
  63.9 83.2 all-gather.8
  157.3 31.9 all-reduce.6
  190.7 24.2 all-gather.14
  217.7 31.9 all-reduce.8
  251.2 25.5 all-gather.18
  278.9 25.5 all-gather.16
  361.5 59.1 all-reduce.10
  423.1 33.9 reduce-scatter.1
  459.2 226.7 all-gather.20
